TPU v7x, 32 devices: a whole 2x2x4 slice. The times are simulated.
32 devices in a mesh: dp: 16 (over z, x, core), mp: 2 (over y).
Axes of the slice: x: 2, y: 2, z: 4, core: 2. Of those that a mesh axis runs over, the one named last changes fastest.
Arguments:
- ranges: bfloat16 [512, 2652], P(('dp', 'mp')), may hold values from 0.0099487305 to 1
- board: int32 [512, 5], P(('dp', 'mp')), may hold values from 0 to 51, as said below
- targets: bfloat16 [512, 2652], P(('dp', 'mp')), may hold values from -6 to 6
- w_in: bfloat16 [1536, 2704], P(('mp', 'dp')), may hold values from -0.34570312 to 0.34570312
- w_out: bfloat16 [1536, 2652], P(('mp', 'dp')), may hold values from -0.3046875 to 0.3046875
Outputs:
- predicted: bfloat16 [512, 2652], P(('dp', 'mp'))
- update_in: float32 [1536, 2704], P(('mp', 'dp'))
- update_out: float32 [1536, 2652], P(('mp', 'dp'))
- loss: float32 [], replicated
Inputs may be any that keep to these rules, and one draw needn't show every extreme that they name: `board`: each row holds 5 different cards.
All inputs are finite; a program needn't handle non-finite values.
Results may differ from a plain program's by a relative error of at most 0.014.
Values may be sent and summed in bfloat16 or wider, within the bound.
No kernel may reach another device: no remote copies, remote signals or barrier semaphores. Data moves between devices by JAX's collectives and lax.ppermute only.
A program may use at most 64 MiB of HBM per device.

v0:
```python
import jax
import jax.numpy as jnp
from jax import lax
from jax.sharding import PartitionSpec as P

CARDS = 52
HIDDEN_SIZE = 1536


def huber_terms(error_value):
    magnitude = jnp.abs(error_value)
    return jnp.where(magnitude <= 1.0, 0.5 * error_value * error_value, magnitude - 0.5)


def build_features(all_ranges, all_board, card_count):
    card_ids = jnp.arange(card_count, dtype=jnp.int32)
    onehot_board = jnp.sum(
        (all_board[:, :, None] == card_ids[None, None, :]).astype(jnp.float32), axis=1
    ).astype(jnp.bfloat16)
    return jnp.concatenate([all_ranges, onehot_board], axis=1)


def right_product(left_side, right_block):
    return lax.dot_general(
        left_side, right_block, (((1,), (1,)), ((), ())), preferred_element_type=jnp.float32
    )


def left_product(left_side, right_side):
    return lax.dot_general(
        left_side, right_side, (((0,), (0,)), ((), ())), preferred_element_type=jnp.float32
    )


def body(ranges, board, targets, w_in, w_out):
    mp_count = lax.axis_size("mp")
    dp_count = lax.axis_size("dp")
    stored_rows = ranges.shape[0]
    value_width = w_out.shape[1]
    all_ranges, all_board = (
        lax.all_gather(ranges, "mp", axis=0, tiled=True),
        lax.all_gather(board, "mp", axis=0, tiled=True),
    )
    features = build_features(all_ranges, all_board, CARDS)
    local_in = lax.all_gather(w_in, "dp", axis=0, tiled=True)
    preact = right_product(features, local_in)
    hidden = jax.nn.gelu(preact).astype(jnp.bfloat16)
    local_out = lax.all_gather(w_out, "dp", axis=0, tiled=True)
    partial_value = jnp.dot(hidden, local_out, preferred_element_type=jnp.float32)
    stacked = partial_value.astype(jnp.bfloat16).reshape(mp_count, stored_rows, value_width)
    received = lax.all_to_all(stacked, "mp", split_axis=0, concat_axis=0, tiled=True)
    summed = jnp.sum(received.astype(jnp.float32), axis=0)
    error_value = summed - targets.astype(jnp.float32)
    own_grad = jnp.clip(error_value, -1.0, 1.0).astype(jnp.bfloat16)
    out_grad = lax.all_gather(own_grad, "mp", axis=0, tiled=True)
    predicted = summed.astype(jnp.bfloat16)
    loss_part = jnp.sum(huber_terms(error_value))
    loss_total = lax.psum(loss_part, ("dp", "mp"))
    grad_out = lax.psum_scatter(
        left_product(hidden, out_grad), "dp", scatter_dimension=0, tiled=True
    )
    back_out = lax.all_gather(w_out, "dp", axis=0, tiled=True)
    hidden_grad = right_product(out_grad, back_out)
    unused_value, gelu_back = jax.vjp(jax.nn.gelu, preact)
    preact_grad = gelu_back(hidden_grad)[0].astype(jnp.bfloat16)
    grad_in = lax.psum_scatter(
        left_product(preact_grad, features), "dp", scatter_dimension=0, tiled=True
    )
    square_part = jnp.sum(grad_in * grad_in) + jnp.sum(grad_out * grad_out)
    square_total = lax.psum(square_part, ("dp", "mp"))
    count_params = HIDDEN_SIZE * (w_in.shape[1] + value_width)
    scale = lax.rsqrt(square_total / count_params + 1e-06)
    loss = loss_total / (stored_rows * mp_count * dp_count * value_width)
    return (predicted, grad_in * scale, grad_out * scale, loss)


def solution(mesh):
    in_specs = (
        P(("dp", "mp"), None),
        P(("dp", "mp"), None),
        P(("dp", "mp"), None),
        P(("mp", "dp"), None),
        P(("mp", "dp"), None),
    )
    out_specs = (P(("dp", "mp"), None), P(("mp", "dp"), None), P(("mp", "dp"), None), P())
    return jax.shard_map(body, mesh=mesh, in_specs=in_specs, out_specs=out_specs, check_vma=False)
```

profile of v0, /device:TPU:0, one launch (start us, length us, event | category | flops | bytes accessed | tf_op | source)
XLA Modules:
  0.0 402.8 jit_solution(9901448083366208325)
XLA Ops:
  7.2 0.7 all-gather.4.cloned.1.call-update
  7.9 0.7 all-gather.6.cloned.1.call-update
  8.6 0.0 reduce-scatter.5.cloned.1.call-start
  8.7 5.5 %all-gather = s32[2,16,5]{1,2,0:T(8,128)S(1)} all-gather(s32[1,16,5]{1,2,0:T(8,128)} %bitcast.10), channel_id=1, replica_groups=mesh['dp'=16,'mp'=2] {'mp'}, dimensions={0}, use_global_device_ids=true | all-gather | bytes 960 | tf_op jit(solution)/shard_map/all_gather | solution.py:42
  14.2 0.1 reshape.14
  14.3 5.4 %all_gather.16 = bf16[32,2652]{1,0:T(8,128)(2,1)S(1)} all-gather(bf16[16,2652]{1,0:T(8,128)(2,1)} %param.5), channel_id=1, replica_groups=mesh['dp'=16,'mp'=2] {'mp'}, dimensions={0}, use_global_device_ids=true | all-gather | bytes 254592 | tf_op jit(solution)/shard_map/all_gather | solution.py:41
  19.7 0.1 convert_reduce_fusion.1
  19.8 44.3 %all-gather.4.cloned.1.call-done = bf16[768,2704]{1,0:T(8,128)(2,1)} async-done(((bf16[48,2704]{1,0:T(8,128)(2,1)}), bf16[768,2704]{1,0:T(8,128)(2,1)}) %all-gather.4.cloned.1.call-update) | async-done | bytes 4153360 | tf_op jit(solution)/shard_map/all_gather | solution.py:45
  64.1 3.6 fusion.3
  67.6 47.4 %all-gather.6.cloned.1.call-done = bf16[768,2652]{1,0:T(8,128)(2,1)} async-done(((bf16[48,2652]{1,0:T(8,128)(2,1)}), bf16[768,2652]{1,0:T(8,128)(2,1)}) %all-gather.6.cloned.1.call-update) | async-done | bytes 4073488 | tf_op jit(solution)/shard_map/all_gather | solution.py:48
  115.1 3.0 convolution_convert_fusion
  118.0 7.2 %all_to_all.5 = bf16[2,16,2652]{2,1,0:T(8,128)(2,1)S(1)} all-to-all(bf16[2,16,2652]{2,1,0:T(8,128)(2,1)S(1)} %bitcast.9), channel_id=1, replica_groups=mesh['dp'=16,'mp'=2] {'mp'}, dimensions={0} | all-to-all | bytes 339456 | tf_op jit(solution)/shard_map/all_to_all | solution.py:51
  125.3 1.3 fusion.1
  126.6 5.1 %all_gather.20 = bf16[32,2652]{1,0:T(8,128)(2,1)S(1)} all-gather(bf16[16,2652]{1,0:T(8,128)(2,1)S(1)} %get-tuple-element.7), channel_id=1, replica_groups=mesh['dp'=16,'mp'=2] {'mp'}, dimensions={0}, use_global_device_ids=true | all-gather | bytes 254592 | tf_op jit(solution)/shard_map/all_gather | solution.py:55
  131.8 4.5 %fusion.26 = f32[768,2652]{1,0:T(8,128)} fusion(bf16[32,2652]{1,0:T(8,128)(2,1)S(1)} %all_gather.20, f32[32,768]{1,0:T(8,128)S(1)} %fusion.3), kind=kOutput, calls=%fused_computation.40 | convolution fusion | flops 130572288 | bytes 8414976 | tf_op jit(solution)/shard_map/dot_general | solution.py:30
  136.2 0.0 reduce-scatter.3.cloned.1.call-start
  136.3 9.1 %fusion.2 = f32[768,2704]{1,0:T(8,128)} fusion(bf16[32,52]{1,0:T(8,128)(2,1)S(1)} %convert_reduce_fusion.1, bf16[32,2652]{1,0:T(8,128)(2,1)S(1)} %all_gather.16, f32[32,768]{1,0:T(8,128)S(1)} %fusion.3, bf16[32,2652]{1,0:T(8,128)(2,1)S(1)} %all_gather.20, bf16[768,2652]{1,0:T(8,128)(2,1)} %all-gather.6.cloned.1.call-done), kind=kOutput, calls=%fused_computation.14 | convolution fusion | flops 264095744 | bytes 12821248 | tf_op jit(solution)/shard_map/dot_general | solution.py:30
  145.5 91.6 %reduce-scatter.5.cloned.1.call-done = f32[48,2652]{1,0:T(8,128)} async-done(((f32[768,2652]{1,0:T(8,128)}), f32[48,2652]{1,0:T(8,128)}) %reduce-scatter.5.cloned.1.call-update) | async-done | bytes 509200 | tf_op jit(solution)/shard_map/reduce_scatter | solution.py:59
  237.0 1.8 multiply_reduce_fusion.1
  238.8 107.6 %reduce-scatter.3.cloned.1.call-done = f32[48,2704]{1,0:T(8,128)} async-done(((f32[768,2704]{1,0:T(8,128)}), f32[48,2704]{1,0:T(8,128)}) %reduce-scatter.3.cloned.1.call-update) | async-done | bytes 519184 | tf_op jit(solution)/shard_map/reduce_scatter | solution.py:66
  346.4 1.8 multiply_reduce_fusion
  349.5 40.5 %all-reduce = (f32[]{:T(128)}, f32[]{:T(128)}) all-reduce(f32[]{:T(128)S(6)} %add.26, f32[]{:T(128)} %get-tuple-element.6), channel_id=1, replica_groups=mesh['dp'=16,'mp'=2] {'dp','mp'}, use_global_device_ids=true, to_apply=%region_6.7 | all-reduce | flops 2 | bytes 16 | tf_op jit(solution)/shard_map/psum | solution.py:70
  391.4 1.9 broadcast_multiply_fusion.1
  393.3 1.9 broadcast_multiply_fusion
  (8 shorter events, 0.1 us)
Async XLA Ops:
  7.2 56.9 %all-gather.4.cloned.1.call-start = ((), (), s32[]{:S(2)}) async-start(), calls=%async_computation.3 | async-start | bytes 4595712 | tf_op jit(solution)/shard_map/all_gather | solution.py:45
  7.9 107.2 %all-gather.6.cloned.1.call-start = ((), (), s32[]{:S(2)}) async-start(), calls=%async_computation.4 | async-start | bytes 4386816 | tf_op jit(solution)/shard_map/all_gather | solution.py:48
  8.6 228.4 %reduce-scatter.5.cloned.1.call-start = ((), (), s32[]{:S(2)}) async-start(), calls=%async_computation.6 | async-start | bytes 8773632 | tf_op jit(solution)/shard_map/reduce_scatter | solution.py:59
  19.7 105.6 %copy-start = (bf16[16,2652]{1,0:T(8,128)(2,1)S(1)}, bf16[16,2652]{1,0:T(8,128)(2,1)}, u32[]{:S(2)}) copy-start(bf16[16,2652]{1,0:T(8,128)(2,1)} %param.7) | copy-start | bytes 254596
  136.2 210.2 %reduce-scatter.3.cloned.1.call-start = ((), (), s32[]{:S(2)}) async-start(), calls=%async_computation.5 | async-start | bytes 9191424 | tf_op jit(solution)/shard_map/reduce_scatter | solution.py:66
Sparse Core Ops, SparseCore 0:
  10.3 53.7 all-gather.3
  66.4 48.6 all-gather.5
  136.4 100.6 reduce-scatter.4
  241.0 105.4 reduce-scatter.2
where the time goes:
time: 403 us
  waiting for transfers between devices  292 us (72%)
  blocking collectives  63.8 us (16%)
  matrix products  20.1 us (5%)
  between operations  17.6 us (4%)
  other arithmetic  8.71 us (2%)
    reduce_scatter x1, waiting for transfers between devices, body(): lax.psum_scatter(left_product(preact_grad, features), 'dp', scatter_dimen...  108 us
    reduce_scatter x1, waiting for transfers between devices, body(): lax.psum_scatter(left_product(hidden, out_grad), 'dp', scatter_dimension=...  91.6 us
    all_gather x1, waiting for transfers between devices, body(): local_out = lax.all_gather(w_out, 'dp', axis=0, tiled=True)  47.4 us
    all_gather x1, waiting for transfers between devices, body(): local_in = lax.all_gather(w_in, 'dp', axis=0, tiled=True)  44.3 us
    psum x1, blocking collectives, body(): square_total = lax.psum(square_part, ('dp', 'mp'))  40.5 us
    dot_general x2, matrix products, left_product(): lax.dot_general(left_side, right_side, (((0,), (0,)), ((), ())), preferre...  13.6 us
  transfers between devices with their start and end apart: 4, of which 4 were waited for; matrix products, arithmetic and copies ran while one was open for 4% of the time, Pallas kernels for 0%

commit v1 on v0

--- a/solution.py
+++ b/solution.py
@@ -45,7 +45,13 @@
     local_in = lax.all_gather(w_in, "dp", axis=0, tiled=True)
     preact = right_product(features, local_in)
     hidden = jax.nn.gelu(preact).astype(jnp.bfloat16)
-    local_out = lax.all_gather(w_out, "dp", axis=0, tiled=True)
+    peers = lax.axis_size("dp")
+    moving, shards = (w_out, [w_out])
+    for _ in range(peers - 1):
+        moving = lax.ppermute(moving, "dp", [(i, (i + 1) % peers) for i in range(peers)])
+        shards.insert(0, moving)
+    flat = jnp.concatenate(shards, axis=0)
+    local_out = jnp.roll(flat, (lax.axis_index("dp") + 1) * w_out.shape[0], axis=0)
     partial_value = jnp.dot(hidden, local_out, preferred_element_type=jnp.float32)
     stacked = partial_value.astype(jnp.bfloat16).reshape(mp_count, stored_rows, value_width)
     received = lax.all_to_all(stacked, "mp", split_axis=0, concat_axis=0, tiled=True)

time: 403 us -> 470 us (1.17)
  waiting for transfers between devices: 292 us -> 328 us
  local copies, waits for them, and re-layouts: 0.09 us -> 30.3 us
    ppermute x0 -> x15, waiting for transfers between devices: none -> 130 us  [body(): lax.ppermute(moving, 'dp', [(i, (i + 1) % peers) for i in range(peers)])]
    all_gather x1, waiting for transfers between devices: 47.4 us -> 0.02 us  [body(): back_out = lax.all_gather(w_out, 'dp', axis=0, tiled=True)]
    all_gather x1, waiting for transfers between devices: 44.3 us -> 0.01 us  [body(): local_in = lax.all_gather(w_in, 'dp', axis=0, tiled=True)]
    unnamed x3 -> x44, local copies, waits for them, and re-layouts: 0.09 us -> 29.5 us
  transfers between devices with their start and end apart: 4 -> 19, of which waited for: 4 -> 16; matrix products, arithmetic and copies ran while one was open for 4% -> 11% of each run, Pallas kernels for 0% -> 0%
where the time goes in v1:
time: 470 us; the launch traced here: 469 us
  waiting for transfers between devices  328 us (70%)
  blocking collectives  62.9 us (13%)
  local copies, waits for them, and re-layouts  30.3 us (6%)
  matrix products  21 us (4%)
  between operations  17.6 us (4%)
  other arithmetic  8.71 us (2%)
    ppermute x15, waiting for transfers between devices, body(): lax.ppermute(moving, 'dp', [(i, (i + 1) % peers) for i in range(peers)])  130 us
    reduce_scatter x1, waiting for transfers between devices, body(): lax.psum_scatter(left_product(preact_grad, features), 'dp', scatter_dimen...  108 us
    reduce_scatter x1, waiting for transfers between devices, body(): lax.psum_scatter(left_product(hidden, out_grad), 'dp', scatter_dimension=...  89.4 us
    psum x1, blocking collectives, body(): square_total = lax.psum(square_part, ('dp', 'mp'))  40.5 us
    unnamed x44, local copies, waits for them, and re-layouts  29.5 us
    dot_general x2, matrix products, left_product(): lax.dot_general(left_side, right_side, (((0,), (0,)), ((), ())), preferre...  14 us
  transfers between devices with their start and end apart: 19, of which 16 were waited for; matrix products, arithmetic and copies ran while one was open for 11% of the time, Pallas kernels for 0%

profile of v1, /device:TPU:0, one launch (start us, length us, event | category | flops | bytes accessed | tf_op | source)
XLA Modules:
  0.0 468.9 jit_solution(7050164687897728553)
XLA Ops:
  8.5 9.2 %collective-permute-done = bf16[48,2652]{1,0:T(8,128)(2,1)S(1)} collective-permute-done((bf16[48,2652]{1,0:T(8,128)(2,1)}, bf16[48,2652]{1,0:T(8,128)(2,1)S(1)}, u32[]{:S(2)}, u32[]{:S(2)}) %collective-permute-start) | collective-permute-done | bytes 254624 | tf_op jit(solution)/shard_map/ppermute | solution.py:51
  17.7 8.6 %collective-permute-done.1 = bf16[48,2652]{1,0:T(8,128)(2,1)S(1)} collective-permute-done((bf16[48,2652]{1,0:T(8,128)(2,1)S(1)}, bf16[48,2652]{1,0:T(8,128)(2,1)S(1)}, u32[]{:S(2)}, u32[]{:S(2)}) %collective-permute-start.1) | collective-permute-done | bytes 254624 | tf_op jit(solution)/shard_map/ppermute | solution.py:51
  26.3 11.8 %collective-permute-done.2 = bf16[48,2652]{1,0:T(8,128)(2,1)S(1)} collective-permute-done((bf16[48,2652]{1,0:T(8,128)(2,1)S(1)}, bf16[48,2652]{1,0:T(8,128)(2,1)S(1)}, u32[]{:S(2)}, u32[]{:S(2)}) %collective-permute-start.2) | collective-permute-done | bytes 254624 | tf_op jit(solution)/shard_map/ppermute | solution.py:51
  38.0 9.1 %collective-permute-done.3 = bf16[48,2652]{1,0:T(8,128)(2,1)S(1)} collective-permute-done((bf16[48,2652]{1,0:T(8,128)(2,1)S(1)}, bf16[48,2652]{1,0:T(8,128)(2,1)S(1)}, u32[]{:S(2)}, u32[]{:S(2)}) %collective-permute-start.3) | collective-permute-done | bytes 254624 | tf_op jit(solution)/shard_map/ppermute | solution.py:51
  47.1 13.2 %collective-permute-done.4 = bf16[48,2652]{1,0:T(8,128)(2,1)S(1)} collective-permute-done((bf16[48,2652]{1,0:T(8,128)(2,1)S(1)}, bf16[48,2652]{1,0:T(8,128)(2,1)S(1)}, u32[]{:S(2)}, u32[]{:S(2)}) %collective-permute-start.4) | collective-permute-done | bytes 254624 | tf_op jit(solution)/shard_map/ppermute | solution.py:51
  60.4 10.2 %collective-permute-done.5 = bf16[48,2652]{1,0:T(8,128)(2,1)S(1)} collective-permute-done((bf16[48,2652]{1,0:T(8,128)(2,1)S(1)}, bf16[48,2652]{1,0:T(8,128)(2,1)S(1)}, u32[]{:S(2)}, u32[]{:S(2)}) %collective-permute-start.5) | collective-permute-done | bytes 254624 | tf_op jit(solution)/shard_map/ppermute | solution.py:51
  70.6 8.4 %collective-permute-done.6 = bf16[48,2652]{1,0:T(8,128)(2,1)S(1)} collective-permute-done((bf16[48,2652]{1,0:T(8,128)(2,1)S(1)}, bf16[48,2652]{1,0:T(8,128)(2,1)S(1)}, u32[]{:S(2)}, u32[]{:S(2)}) %collective-permute-start.6) | collective-permute-done | bytes 254624 | tf_op jit(solution)/shard_map/ppermute | solution.py:51
  79.1 8.4 %collective-permute-done.7 = bf16[48,2652]{1,0:T(8,128)(2,1)S(1)} collective-permute-done((bf16[48,2652]{1,0:T(8,128)(2,1)S(1)}, bf16[48,2652]{1,0:T(8,128)(2,1)S(1)}, u32[]{:S(2)}, u32[]{:S(2)}) %collective-permute-start.7) | collective-permute-done | bytes 254624 | tf_op jit(solution)/shard_map/ppermute | solution.py:51
  87.5 8.4 %collective-permute-done.8 = bf16[48,2652]{1,0:T(8,128)(2,1)S(1)} collective-permute-done((bf16[48,2652]{1,0:T(8,128)(2,1)S(1)}, bf16[48,2652]{1,0:T(8,128)(2,1)S(1)}, u32[]{:S(2)}, u32[]{:S(2)}) %collective-permute-start.8) | collective-permute-done | bytes 254624 | tf_op jit(solution)/shard_map/ppermute | solution.py:51
  96.0 8.4 %collective-permute-done.9 = bf16[48,2652]{1,0:T(8,128)(2,1)S(1)} collective-permute-done((bf16[48,2652]{1,0:T(8,128)(2,1)S(1)}, bf16[48,2652]{1,0:T(8,128)(2,1)S(1)}, u32[]{:S(2)}, u32[]{:S(2)}) %collective-permute-start.9) | collective-permute-done | bytes 254624 | tf_op jit(solution)/shard_map/ppermute | solution.py:51
  104.4 8.4 %collective-permute-done.10 = bf16[48,2652]{1,0:T(8,128)(2,1)S(1)} collective-permute-done((bf16[48,2652]{1,0:T(8,128)(2,1)S(1)}, bf16[48,2652]{1,0:T(8,128)(2,1)S(1)}, u32[]{:S(2)}, u32[]{:S(2)}) %collective-permute-start.10) | collective-permute-done | bytes 254624 | tf_op jit(solution)/shard_map/ppermute | solution.py:51
  112.9 8.4 %collective-permute-done.11 = bf16[48,2652]{1,0:T(8,128)(2,1)S(1)} collective-permute-done((bf16[48,2652]{1,0:T(8,128)(2,1)S(1)}, bf16[48,2652]{1,0:T(8,128)(2,1)S(1)}, u32[]{:S(2)}, u32[]{:S(2)}) %collective-permute-start.11) | collective-permute-done | bytes 254624 | tf_op jit(solution)/shard_map/ppermute | solution.py:51
  122.0 8.4 %collective-permute-done.12 = bf16[48,2652]{1,0:T(8,128)(2,1)S(1)} collective-permute-done((bf16[48,2652]{1,0:T(8,128)(2,1)S(1)}, bf16[48,2652]{1,0:T(8,128)(2,1)S(1)}, u32[]{:S(2)}, u32[]{:S(2)}) %collective-permute-start.12) | collective-permute-done | bytes 254624 | tf_op jit(solution)/shard_map/ppermute | solution.py:51
  131.2 8.6 %collective-permute-done.13 = bf16[48,2652]{1,0:T(8,128)(2,1)} collective-permute-done((bf16[48,2652]{1,0:T(8,128)(2,1)S(1)}, bf16[48,2652]{1,0:T(8,128)(2,1)}, u32[]{:S(2)}, u32[]{:S(2)}) %collective-permute-start.13) | collective-permute-done | bytes 254624 | tf_op jit(solution)/shard_map/ppermute | solution.py:51
  139.8 4.5 all-gather
  144.4 5.5 %all_gather.15 = bf16[32,2652]{1,0:T(8,128)(2,1)S(1)} all-gather(bf16[16,2652]{1,0:T(8,128)(2,1)} %param.5), channel_id=1, replica_groups=mesh['dp'=16,'mp'=2] {'mp'}, dimensions={0}, use_global_device_ids=true | all-gather | bytes 254592 | tf_op jit(solution)/shard_map/all_gather | solution.py:41
  178.8 3.6 fusion.8
  185.9 7.2 %all_to_all.5 = bf16[2,16,2652]{2,1,0:T(8,128)(2,1)S(1)} all-to-all(bf16[2,16,2652]{2,1,0:T(8,128)(2,1)S(1)} %bitcast.8), channel_id=1, replica_groups=mesh['dp'=16,'mp'=2] {'mp'}, dimensions={0} | all-to-all | bytes 339456 | tf_op jit(solution)/shard_map/all_to_all | solution.py:57
  194.4 5.1 %all_gather.18 = bf16[32,2652]{1,0:T(8,128)(2,1)S(1)} all-gather(bf16[16,2652]{1,0:T(8,128)(2,1)S(1)} %get-tuple-element.7), channel_id=1, replica_groups=mesh['dp'=16,'mp'=2] {'mp'}, dimensions={0}, use_global_device_ids=true | all-gather | bytes 254592 | tf_op jit(solution)/shard_map/all_gather | solution.py:61
  199.6 4.5 fusion.32
  204.2 9.5 %fusion.7 = f32[768,2704]{1,0:T(8,128)} fusion(bf16[32,52]{1,0:T(8,128)(2,1)S(1)} %convert_reduce_fusion.1, bf16[32,2652]{1,0:T(8,128)(2,1)S(1)} %all_gather.15, f32[32,768]{1,0:T(8,128)S(1)} %fusion.8, bf16[32,2652]{1,0:T(8,128)(2,1)S(1)} %all_gather.18, bf16[768,2652]{1,0:T(8,128)(2,1)} %all-gather.6.cloned.1.call-done), kind=kOutput, calls=%fused_computation.16 | convolution fusion | flops 264095744 | bytes 12821248 | tf_op jit(solution)/shard_map/dot_general | solution.py:30
  213.7 89.4 %reduce-scatter.5.cloned.1.call-done = f32[48,2652]{1,0:T(8,128)} async-done(((f32[768,2652]{1,0:T(8,128)}), f32[48,2652]{1,0:T(8,128)}) %reduce-scatter.5.cloned.1.call-update) | async-done | bytes 509200 | tf_op jit(solution)/shard_map/reduce_scatter | solution.py:65
  304.9 107.7 %reduce-scatter.3.cloned.1.call-done = f32[48,2704]{1,0:T(8,128)} async-done(((f32[768,2704]{1,0:T(8,128)}), f32[48,2704]{1,0:T(8,128)}) %reduce-scatter.3.cloned.1.call-update) | async-done | bytes 519184 | tf_op jit(solution)/shard_map/reduce_scatter | solution.py:72
  415.6 40.5 %all-reduce = (f32[]{:T(128)}, f32[]{:T(128)}) all-reduce(f32[]{:T(128)S(6)} %add.42, f32[]{:T(128)} %get-tuple-element.6), channel_id=1, replica_groups=mesh['dp'=16,'mp'=2] {'dp','mp'}, use_global_device_ids=true, to_apply=%region_6.7 | all-reduce | flops 2 | bytes 16 | tf_op jit(solution)/shard_map/psum | solution.py:76
  (80 shorter events, 44.0 us)
Async XLA Ops:
  7.2 157.4 %copy-start = (bf16[48,2652]{1,0:T(8,128)(2,1)S(1)}, bf16[48,2652]{1,0:T(8,128)(2,1)}, u32[]{:S(2)}) copy-start(bf16[48,2652]{1,0:T(8,128)(2,1)} %param.9) | copy-start | bytes 763780
  7.2 171.6 %all-gather.4.cloned.1.call-start = ((), (), s32[]{:S(2)}) async-start(), calls=%async_computation.3 | async-start | bytes 4595712 | tf_op jit(solution)/shard_map/all_gather | solution.py:45
  7.9 196.3 %all-gather.6.cloned.1.call-start = ((), (), s32[]{:S(2)}) async-start(), calls=%async_computation.4 | async-start | bytes 4386816 | tf_op jit(solution)/shard_map/all_gather | solution.py:68
  8.0 9.7 %collective-permute-start = (bf16[48,2652]{1,0:T(8,128)(2,1)}, bf16[48,2652]{1,0:T(8,128)(2,1)S(1)}, u32[]{:S(2)}, u32[]{:S(2)}) collective-permute-start(bf16[48,2652]{1,0:T(8,128)(2,1)} %param.9), channel_id=1, source_target_pairs={{0,2},{2,4},{4,6},{6,8},{8,10},{10,12},{12,14},{14,16},{16,18},{18... | collective-permute-start | bytes 763784 | tf_op jit(solution)/shard_map/ppermute | solution.py:51
  17.7 8.6 %collective-permute-start.1 = (bf16[48,2652]{1,0:T(8,128)(2,1)S(1)}, bf16[48,2652]{1,0:T(8,128)(2,1)S(1)}, u32[]{:S(2)}, u32[]{:S(2)}) collective-permute-start(bf16[48,2652]{1,0:T(8,128)(2,1)S(1)} %collective-permute-done), channel_id=1, source_target_pairs={{0,2},{2,4},{4,6},{6,8},{8,10},{10,12},{12,14},{14,16},{16,18},{18... | collective-permute-start | bytes 763784 | tf_op jit(solution)/shard_map/ppermute | solution.py:51
  26.3 11.8 %collective-permute-start.2 = (bf16[48,2652]{1,0:T(8,128)(2,1)S(1)}, bf16[48,2652]{1,0:T(8,128)(2,1)S(1)}, u32[]{:S(2)}, u32[]{:S(2)}) collective-permute-start(bf16[48,2652]{1,0:T(8,128)(2,1)S(1)} %collective-permute-done.1), channel_id=1, source_target_pairs={{0,2},{2,4},{4,6},{6,8},{8,10},{10,12},{12,14},{14,16},{16,18},{18... | collective-permute-start | bytes 763784 | tf_op jit(solution)/shard_map/ppermute | solution.py:51
  38.0 9.1 %collective-permute-start.3 = (bf16[48,2652]{1,0:T(8,128)(2,1)S(1)}, bf16[48,2652]{1,0:T(8,128)(2,1)S(1)}, u32[]{:S(2)}, u32[]{:S(2)}) collective-permute-start(bf16[48,2652]{1,0:T(8,128)(2,1)S(1)} %collective-permute-done.2), channel_id=1, source_target_pairs={{0,2},{2,4},{4,6},{6,8},{8,10},{10,12},{12,14},{14,16},{16,18},{18... | collective-permute-start | bytes 763784 | tf_op jit(solution)/shard_map/ppermute | solution.py:51
  47.1 13.2 %collective-permute-start.4 = (bf16[48,2652]{1,0:T(8,128)(2,1)S(1)}, bf16[48,2652]{1,0:T(8,128)(2,1)S(1)}, u32[]{:S(2)}, u32[]{:S(2)}) collective-permute-start(bf16[48,2652]{1,0:T(8,128)(2,1)S(1)} %collective-permute-done.3), channel_id=1, source_target_pairs={{0,2},{2,4},{4,6},{6,8},{8,10},{10,12},{12,14},{14,16},{16,18},{18... | collective-permute-start | bytes 763784 | tf_op jit(solution)/shard_map/ppermute | solution.py:51
  60.4 10.2 %collective-permute-start.5 = (bf16[48,2652]{1,0:T(8,128)(2,1)S(1)}, bf16[48,2652]{1,0:T(8,128)(2,1)S(1)}, u32[]{:S(2)}, u32[]{:S(2)}) collective-permute-start(bf16[48,2652]{1,0:T(8,128)(2,1)S(1)} %collective-permute-done.4), channel_id=1, source_target_pairs={{0,2},{2,4},{4,6},{6,8},{8,10},{10,12},{12,14},{14,16},{16,18},{18... | collective-permute-start | bytes 763784 | tf_op jit(solution)/shard_map/ppermute | solution.py:51
  70.6 8.5 %collective-permute-start.6 = (bf16[48,2652]{1,0:T(8,128)(2,1)S(1)}, bf16[48,2652]{1,0:T(8,128)(2,1)S(1)}, u32[]{:S(2)}, u32[]{:S(2)}) collective-permute-start(bf16[48,2652]{1,0:T(8,128)(2,1)S(1)} %collective-permute-done.5), channel_id=1, source_target_pairs={{0,2},{2,4},{4,6},{6,8},{8,10},{10,12},{12,14},{14,16},{16,18},{18... | collective-permute-start | bytes 763784 | tf_op jit(solution)/shard_map/ppermute | solution.py:51
  79.1 8.5 %collective-permute-start.7 = (bf16[48,2652]{1,0:T(8,128)(2,1)S(1)}, bf16[48,2652]{1,0:T(8,128)(2,1)S(1)}, u32[]{:S(2)}, u32[]{:S(2)}) collective-permute-start(bf16[48,2652]{1,0:T(8,128)(2,1)S(1)} %collective-permute-done.6), channel_id=1, source_target_pairs={{0,2},{2,4},{4,6},{6,8},{8,10},{10,12},{12,14},{14,16},{16,18},{18... | collective-permute-start | bytes 763784 | tf_op jit(solution)/shard_map/ppermute | solution.py:51
  87.5 8.5 %collective-permute-start.8 = (bf16[48,2652]{1,0:T(8,128)(2,1)S(1)}, bf16[48,2652]{1,0:T(8,128)(2,1)S(1)}, u32[]{:S(2)}, u32[]{:S(2)}) collective-permute-start(bf16[48,2652]{1,0:T(8,128)(2,1)S(1)} %collective-permute-done.7), channel_id=1, source_target_pairs={{0,2},{2,4},{4,6},{6,8},{8,10},{10,12},{12,14},{14,16},{16,18},{18... | collective-permute-start | bytes 763784 | tf_op jit(solution)/shard_map/ppermute | solution.py:51
  96.0 8.5 %collective-permute-start.9 = (bf16[48,2652]{1,0:T(8,128)(2,1)S(1)}, bf16[48,2652]{1,0:T(8,128)(2,1)S(1)}, u32[]{:S(2)}, u32[]{:S(2)}) collective-permute-start(bf16[48,2652]{1,0:T(8,128)(2,1)S(1)} %collective-permute-done.8), channel_id=1, source_target_pairs={{0,2},{2,4},{4,6},{6,8},{8,10},{10,12},{12,14},{14,16},{16,18},{18... | collective-permute-start | bytes 763784 | tf_op jit(solution)/shard_map/ppermute | solution.py:51
  104.4 8.5 %collective-permute-start.10 = (bf16[48,2652]{1,0:T(8,128)(2,1)S(1)}, bf16[48,2652]{1,0:T(8,128)(2,1)S(1)}, u32[]{:S(2)}, u32[]{:S(2)}) collective-permute-start(bf16[48,2652]{1,0:T(8,128)(2,1)S(1)} %collective-permute-done.9), channel_id=1, source_target_pairs={{0,2},{2,4},{4,6},{6,8},{8,10},{10,12},{12,14},{14,16},{16,18},{18... | collective-permute-start | bytes 763784 | tf_op jit(solution)/shard_map/ppermute | solution.py:51
  112.9 8.5 %collective-permute-start.11 = (bf16[48,2652]{1,0:T(8,128)(2,1)S(1)}, bf16[48,2652]{1,0:T(8,128)(2,1)S(1)}, u32[]{:S(2)}, u32[]{:S(2)}) collective-permute-start(bf16[48,2652]{1,0:T(8,128)(2,1)S(1)} %collective-permute-done.10), channel_id=1, source_target_pairs={{0,2},{2,4},{4,6},{6,8},{8,10},{10,12},{12,14},{14,16},{16,18},{18... | collective-permute-start | bytes 763784 | tf_op jit(solution)/shard_map/ppermute | solution.py:51
  122.0 8.5 %collective-permute-start.12 = (bf16[48,2652]{1,0:T(8,128)(2,1)S(1)}, bf16[48,2652]{1,0:T(8,128)(2,1)S(1)}, u32[]{:S(2)}, u32[]{:S(2)}) collective-permute-start(bf16[48,2652]{1,0:T(8,128)(2,1)S(1)} %collective-permute-done.11), channel_id=1, source_target_pairs={{0,2},{2,4},{4,6},{6,8},{8,10},{10,12},{12,14},{14,16},{16,18},{18... | collective-permute-start | bytes 763784 | tf_op jit(solution)/shard_map/ppermute | solution.py:51
  130.5 0.7 copy-start.3
  131.2 8.6 %collective-permute-start.13 = (bf16[48,2652]{1,0:T(8,128)(2,1)S(1)}, bf16[48,2652]{1,0:T(8,128)(2,1)}, u32[]{:S(2)}, u32[]{:S(2)}) collective-permute-start(bf16[48,2652]{1,0:T(8,128)(2,1)S(1)} %collective-permute-done.12), channel_id=1, source_target_pairs={{0,2},{2,4},{4,6},{6,8},{8,10},{10,12},{12,14},{14,16},{16,18},{18... | collective-permute-start | bytes 763784 | tf_op jit(solution)/shard_map/ppermute | solution.py:51
  139.7 10.3 %collective-permute-start.14 = (bf16[48,2652]{1,0:T(8,128)(2,1)}, bf16[48,2652]{1,0:T(8,128)(2,1)}, u32[]{:S(2)}, u32[]{:S(2)}) collective-permute-start(bf16[48,2652]{1,0:T(8,128)(2,1)} %collective-permute-done.13), channel_id=1, source_target_pairs={{0,2},{2,4},{4,6},{6,8},{8,10},{10,12},{12,14},{14,16},{16,18},{18... | collective-permute-start | bytes 763784 | tf_op jit(solution)/shard_map/ppermute | solution.py:51
  139.7 163.4 %reduce-scatter.5.cloned.1.call-start = ((), (), s32[]{:S(2)}) async-start(), calls=%async_computation.6 | async-start | bytes 8773632 | tf_op jit(solution)/shard_map/reduce_scatter | solution.py:65
  144.4 24.2 %copy-start.4 = (bf16[48,2652]{1,0:T(8,128)(2,1)S(1)}, bf16[48,2652]{1,0:T(8,128)(2,1)}, u32[]{:S(2)}) copy-start(bf16[48,2652]{1,0:T(8,128)(2,1)} %copy-done.3) | copy-start | bytes 763780
  144.4 25.0 %copy-start.2 = (bf16[48,2652]{1,0:T(8,128)(2,1)S(1)}, bf16[48,2652]{1,0:T(8,128)(2,1)}, u32[]{:S(2)}) copy-start(bf16[48,2652]{1,0:T(8,128)(2,1)} %copy-done.1) | copy-start | bytes 763780
  169.4 23.8 %copy-start.5 = (bf16[16,2652]{1,0:T(8,128)(2,1)S(1)}, bf16[16,2652]{1,0:T(8,128)(2,1)}, u32[]{:S(2)}) copy-start(bf16[16,2652]{1,0:T(8,128)(2,1)} %param.7) | copy-start | bytes 254596
  204.1 208.4 %reduce-scatter.3.cloned.1.call-start = ((), (), s32[]{:S(2)}) async-start(), calls=%async_computation.5 | async-start | bytes 9191424 | tf_op jit(solution)/shard_map/reduce_scatter | solution.py:72
  (1 other events, 0.7 us)
Sparse Core Ops, SparseCore 0:
  10.3 58.3 all-gather.3
  139.9 51.2 all-gather.5
  204.2 98.8 reduce-scatter.4
  307.0 105.4 reduce-scatter.2
